TPU v7x, 128 devices: a whole 4x4x4 slice. The times are simulated.
128 devices in a mesh: trial: 16 (over y, x_hi, core), feat: 8 (over x_lo, z).
Axes of the slice: x: 4 (x_hi: 2, x_lo: 2; x = x_hi * 2 + x_lo), y: 4, z: 4, core: 2. Of those that a mesh axis runs over, the one named last changes fastest.
Arguments:
- data: bfloat16 [32768, 256, 128], P('trial', 'feat'), may hold values from -2000 to 2000
- rotations: bfloat16 [768, 32768], P('feat', 'trial'), may hold values from -0.046875 to 0.046875
- span_order: int32 [6], replicated, may hold values from 0 to 5, each once
- adjacency: int32 [128, 128], replicated, may hold values from 0 to 1, as said below
- kernel: float32 [9], replicated, may hold values from 0.1 to 1
Outputs:
- enhanced: float32 [768, 256, 128], P('trial', 'feat')
Inputs may be any that keep to these rules, and one draw needn't show every extreme that they name: `adjacency`: symmetric 0/1 matrix with zero diagonal.
All inputs are finite; a program needn't handle non-finite values.
Results may differ from a plain program's by a relative error of at most 0.0003.
Values may be sent and summed in bfloat16 or wider, within the bound.
A program may use at most 128 MiB of HBM per device.

v0:
```python
import functools

import jax
import jax.numpy as jnp
from jax import lax
from jax.sharding import Mesh
from jax.sharding import PartitionSpec as P

TRIAL = ("trial_0", "trial_1", "trial_2")


def by_axis(x, axes):
    return functools.reduce(lax.psum, axes, x)


def with_halo(x, sides, width):
    for axis, dim in sides:
        devices, length = (lax.axis_size(axis), x.shape[dim])
        up = [(i, (i + 1) % devices) for i in range(devices - 1)]
        down = [(j, i) for i, j in up]
        last = lax.slice_in_dim(x, length - width, length, axis=dim)
        initial = lax.slice_in_dim(x, 0, width, axis=dim)
        before = lax.ppermute(last, axis, up)
        after = lax.ppermute(initial, axis, down)
        x = jnp.concatenate([before, x, after], axis=dim)
    return x


def per_device(data, rotations, span_order, adjacency, kernel):
    trial_rows, tdev, sens = data.shape
    flat = data.reshape(trial_rows, tdev * sens)
    trial_count = lax.axis_size(TRIAL)
    rot_all = rotations.shape[0] * lax.axis_size("feat")
    span_count = span_order.shape[0]
    span_rows = rot_all // span_count
    whole = lax.all_gather(rotations, "feat", axis=0, tiled=True)
    ordered = jnp.take(whole.reshape(span_count, span_rows, trial_rows), span_order, axis=0)
    sums = jnp.dot(ordered.reshape(rot_all, trial_rows), flat, preferred_element_type=jnp.float32)
    local_power = jnp.sum(jnp.square(flat.astype(jnp.float32)), axis=0)
    power = by_axis(local_power, TRIAL) / (trial_rows * trial_count)
    owned = rot_all // trial_count
    mine = lax.psum_scatter(sums, TRIAL, scatter_dimension=0, tiled=True)
    score = mine / jnp.sqrt(power + 1e-05)[None, :]
    squared = (score * score).reshape(owned * tdev, sens)
    links = adjacency.astype(jnp.float32)
    degree = jnp.sum(links, axis=1)
    mix = (jnp.eye(sens, dtype=jnp.float32) + links) / (1.0 + degree)[:, None]
    spread = jnp.dot(squared, mix.T, precision=lax.Precision.HIGHEST).reshape(owned, tdev, sens)
    half = kernel.shape[0] // 2
    padded = with_halo(spread, (("feat", 1),), half)
    enhanced = jnp.zeros((owned, tdev, sens), jnp.float32)
    for step in range(kernel.shape[0]):
        enhanced = enhanced + kernel[step] * padded[:, step : step + tdev, :]
    return enhanced


def solution(mesh):
    torus = Mesh(
        mesh.devices.reshape(4, 2, 2, mesh.shape["feat"]), ("trial_0", "trial_1", "trial_2", "feat")
    )
    in_specs = (P(TRIAL, "feat", None), P("feat", TRIAL), P(), P(), P())
    out_specs = P(TRIAL, "feat", None)
    return jax.shard_map(
        per_device, mesh=torus, in_specs=in_specs, out_specs=out_specs, check_vma=False
    )
```

profile of v0, /device:TPU:2, one launch (start us, length us, event | category | flops | bytes accessed | tf_op | source)
XLA Modules:
  0.0 230.0 jit_solution(6074479926668054016)
XLA Ops:
  6.5 0.0 all-gather.2.cloned.1.call-start
  6.5 0.7 all-gather.2.cloned.1.call-update
  7.3 0.0 reduce-scatter.2.cloned.1.call-start
  7.3 0.7 compare_select_fusion
  8.0 0.7 compare_and_fusion
  8.6 46.0 %all-gather.2.cloned.1.call-done = bf16[768,2048]{1,0:T(8,128)(2,1)} async-done(((bf16[96,2048]{1,0:T(8,128)(2,1)}), bf16[768,2048]{1,0:T(8,128)(2,1)}) %all-gather.2.cloned.1.call-update) | async-done | bytes 3145744 | tf_op jit(solution)/shard_map/all_gather | solution.py:36
  54.6 2.6 %gather_fusion = bf16[6,128,2048]{2,1,0:T(8,128)(2,1)S(1)} fusion(bf16[6,128,2048]{2,1,0:T(8,128)(2,1)} %bitcast.25, s32[1024]{0:T(1024)S(1)} %pad_clamp_fusion), kind=kCustom, calls=%fused_computation | custom fusion | bytes 6291480 | tf_op jit(solution)/shard_map/jit(_take)/gather | solution.py:37
  57.3 0.4 broadcast_select_fusion
  57.6 19.5 %fusion = f32[768,4096]{1,0:T(8,128)} fusion(bf16[768,2048]{1,0:T(8,128)(2,1)S(1)} %bitcast.26, bf16[256,8,32,128]{3,2,1,0:T(8,128)(2,1)} %bitcast.24), kind=kOutput, calls=%fused_computation.2 | convolution fusion | flops 12884901888 | bytes 32505856 | tf_op jit(solution)/shard_map/dot_general | solution.py:38
  77.1 0.0 reduce-scatter.2.cloned.1.call-update
  77.2 0.0 copy-start
  77.2 10.3 %multiply_reduce_fusion = f32[32,128]{1,0:T(8,128)S(1)} fusion(bf16[2048,32,128]{2,1,0:T(8,128)(2,1)} %param.5), kind=kLoop, calls=%fused_computation.1 | loop fusion | flops 25161728 | bytes 16793600 | tf_op jit(solution)/shard_map/reduce_sum | solution.py:39
  87.5 0.0 copy-start.1
  87.5 17.0 %psum.21 = f32[4096]{0:T(1024)S(1)} all-reduce(f32[4096]{0:T(1024)S(1)} %bitcast.28), channel_id=1, replica_groups=mesh['trial_0'=4,'trial_1'=2,'trial_2'=2,'feat'=8] {'trial_0'}, use_global_device_ids=true, to_apply=%region_2.3 | all-reduce | flops 4096 | bytes 32768 | tf_op jit(solution)/shard_map/psum | solution.py:13
  104.5 10.4 %psum.22 = f32[4096]{0:T(1024)S(1)} all-reduce(f32[4096]{0:T(1024)S(1)} %psum.21), channel_id=1, replica_groups=mesh['trial_0'=4,'trial_1'=2,'trial_2'=2,'feat'=8] {'trial_1'}, use_global_device_ids=true, to_apply=%region_3.4 | all-reduce | flops 4096 | bytes 32768 | tf_op jit(solution)/shard_map/psum | solution.py:13
  114.9 3.3 %psum.23 = f32[4096]{0:T(1024)S(1)} all-reduce(f32[4096]{0:T(1024)S(1)} %psum.22), channel_id=1, replica_groups=mesh['trial_0'=4,'trial_1'=2,'trial_2'=2,'feat'=8] {'trial_2'}, use_global_device_ids=true, to_apply=%region_4.5 | all-reduce | flops 4096 | bytes 32768 | tf_op jit(solution)/shard_map/psum | solution.py:13
  118.3 0.0 copy-done
  118.3 0.1 convert_reduce_fusion
  118.4 80.7 %reduce-scatter.2.cloned.1.call-done = f32[48,4096]{1,0:T(8,128)} async-done(((f32[768,4096]{1,0:T(8,128)}), f32[48,4096]{1,0:T(8,128)}) %reduce-scatter.2.cloned.1.call-update) | async-done | bytes 786448 | tf_op jit(solution)/shard_map/reduce_scatter | solution.py:42
  199.1 1.2 multiply_bitcast_fusion
  200.3 0.1 copy.7
  200.4 0.9 fusion.25
  201.4 5.7 %collective-permute-start.1 = (f32[48,4,128]{2,1,0:T(4,128)S(1)}, f32[48,4,128]{2,1,0:T(4,128)S(1)}, u32[]{:S(2)}, u32[]{:S(2)}) collective-permute-start(f32[48,4,128]{2,1,0:T(4,128)S(1)} %get-tuple-element.6), channel_id=1, source_target_pairs={{1,0},{2,1},{3,2},{4,3},{5,4},{6,5},{7,6},{9,8},{10,9},{11,10},{12... | collective-permute-start | bytes 294920 | tf_op jit(solution)/shard_map/ppermute | solution.py:24
  207.1 1.9 collective-permute-start
  209.0 0.0 copy-done.1
  209.0 0.7 fusion.33
  209.7 0.0 collective-permute-done.1
  209.7 6.0 %collective-permute-done = f32[48,4,128]{2,1,0:T(4,128)S(1)} collective-permute-done((f32[48,4,128]{2,1,0:T(4,128)S(1)}, f32[48,4,128]{2,1,0:T(4,128)S(1)}, u32[]{:S(2)}, u32[]{:S(2)}) %collective-permute-start) | collective-permute-done | bytes 98336 | tf_op jit(solution)/shard_map/ppermute | solution.py:23
  215.7 7.4 %fusion.6 = f32[48,32,128]{2,1,0:T(8,128)} fusion(f32[48,32,128]{2,1,0:T(8,128)S(1)} %fusion.25, f32[48,4,128]{2,1,0:T(4,128)S(1)} %collective-permute-done.1, f32[48,4,128]{2,1,0:T(4,128)S(1)} %collective-permute-done, f32[]{:T(128)} %bitcast.12, f32[]{:T(128)} %bitcast.11, f32[]{:T(128)} %bitcast.10, f32[]{:T(128)} %bitcast.9, f32[]{:T(128)} %bitcast.8, ...), kind=kLoop, calls=%fused_computation.21 | loop fusion | flops 4915200 | bytes 1769508 | tf_op jit(solution)/shard_map/add | solution.py:53
  (4 shorter events, 0.1 us)
Async XLA Ops:
  6.5 48.1 %all-gather.2.cloned.1.call-start = ((), (), s32[]{:S(2)}) async-start(), calls=%async_computation.1 | async-start | bytes 3538944 | tf_op jit(solution)/shard_map/all_gather | solution.py:36
  7.3 191.8 %reduce-scatter.2.cloned.1.call-start = ((), (), s32[]{:S(2)}) async-start(), calls=%async_computation.2 | async-start | bytes 13369344 | tf_op jit(solution)/shard_map/reduce_scatter | solution.py:42
  77.2 41.1 %copy-start = (s32[128,128]{1,0:T(8,128)S(1)}, s32[128,128]{1,0:T(8,128)}, u32[]{:S(2)}) copy-start(s32[128,128]{1,0:T(8,128)} %param.8) | copy-start | bytes 196612
  87.5 121.5 %copy-start.1 = (f32[9]{0:T(128)S(1)}, f32[9]{0:T(128)}, u32[]{:S(2)}) copy-start(f32[9]{0:T(128)} %param.9) | copy-start | bytes 112
  201.4 8.3 %collective-permute-start.1 = (f32[48,4,128]{2,1,0:T(4,128)S(1)}, f32[48,4,128]{2,1,0:T(4,128)S(1)}, u32[]{:S(2)}, u32[]{:S(2)}) collective-permute-start(f32[48,4,128]{2,1,0:T(4,128)S(1)} %get-tuple-element.6), channel_id=1, source_target_pairs={{1,0},{2,1},{3,2},{4,3},{5,4},{6,5},{7,6},{9,8},{10,9},{11,10},{12... | collective-permute-start | bytes 294920 | tf_op jit(solution)/shard_map/ppermute | solution.py:24
  207.1 8.6 %collective-permute-start = (f32[48,4,128]{2,1,0:T(4,128)S(1)}, f32[48,4,128]{2,1,0:T(4,128)S(1)}, u32[]{:S(2)}, u32[]{:S(2)}) collective-permute-start(f32[48,4,128]{2,1,0:T(4,128)S(1)} %get-tuple-element.5), channel_id=1, source_target_pairs={{0,1},{1,2},{2,3},{3,4},{4,5},{5,6},{6,7},{8,9},{9,10},{10,11},{11... | collective-permute-start | bytes 294920 | tf_op jit(solution)/shard_map/ppermute | solution.py:23
Sparse Core Ops, SparseCore 0:
  9.0 45.5 all-gather.1
  77.3 121.7 reduce-scatter.1
where the time goes:
time: 230 us
  waiting for transfers between devices  133 us (58%)
  blocking collectives  30.8 us (13%)
  other arithmetic  20.7 us (9%)
  matrix products  20.4 us (9%)
  between operations  13.5 us (6%)
  starting transfers between devices  7.68 us (3%)
  local copies, waits for them, and re-layouts  3.5 us (2%)
    reduce_scatter x1, waiting for transfers between devices, per_device(): mine = lax.psum_scatter(sums, TRIAL, scatter_dimension=0, tiled=True)  80.7 us
    all_gather x1, waiting for transfers between devices, per_device(): whole = lax.all_gather(rotations, 'feat', axis=0, tiled=True)  46 us
    psum x3, blocking collectives, by_axis(): return functools.reduce(lax.psum, axes, x)  30.8 us
    dot_general x1, matrix products, per_device(): jnp.dot(ordered.reshape(rot_all, trial_rows), flat, preferred_element_typ...  19.5 us
    reduce_sum x1, other arithmetic, per_device(): local_power = jnp.sum(jnp.square(flat.astype(jnp.float32)), axis=0)  10.3 us
    add x1, other arithmetic, per_device(): enhanced = enhanced + kernel[step] * padded[:, step:step + tdev, :]  7.41 us
    ppermute x1, waiting for transfers between devices, with_halo(): before = lax.ppermute(last, axis, up)  6 us
    ppermute x1, starting transfers between devices, with_halo(): after = lax.ppermute(initial, axis, down)  5.71 us
  transfers between devices with their start and end apart: 4, of which 3 were waited for; matrix products, arithmetic and copies ran while one was open for 5% of the time, Pallas kernels for 0%

commit v1 on v0

v1 whole, which is shorter than its diff:
```python
import functools

import jax
import jax.numpy as jnp
from jax import lax
from jax.experimental import pallas as pl
from jax.experimental.pallas import tpu as pltpu
from jax.sharding import Mesh
from jax.sharding import PartitionSpec as P

TRIAL = ("y", "xh", "c")
FEAT = ("xl", "z")
MESH = pl.DeviceIdType.MESH
F32, BF16, I16 = jnp.float32, jnp.bfloat16, jnp.int16
TOP = 32000.0

TRIALS, TDEV, SENS = 2048, 32, 128
BLOCK, BATCH, OWNED = 96, 384, 48
CHUNK, SLOTS = 128, 4
UNITS = BLOCK // 16
AWAY = ((0, 0), (1, 0), (0, 3), (0, 1), (0, 2), (1, 3), (1, 1), (1, 2))


def encode(v, q_at, s_at):
    top = jnp.maximum(jnp.max(jnp.abs(v), axis=0, keepdims=True), 1e-30)
    q_at(jnp.round(v * (TOP / top)).astype(jnp.int32).astype(I16))
    s_at(top * (1.0 / TOP))


def decode(q, s):
    return q.astype(jnp.int32).astype(F32) * s


def kernel(
    order, taps, data, rot, adj, out,
    raw, dv, rotg, lp, pw, part, part_in, acc,
    s1, s1s, r1, r1s, s2, s2s, r2, r2s, sx, sxs, rx, rxs, fin, place,
    a2s, a2ss, a2r, a2rs, hr, hrs, spread, turn,
    raw_sem, ag_s, ag_r, pw_s, pw_r, d_s, d_r, r1_s, r1_r, r2_s, r2_r, x_s, x_r, a_s, a_r, h_s, h_r,
):
    y, xh, c = lax.axis_index("y"), lax.axis_index("xh"), lax.axis_index("c")
    xl, z = lax.axis_index("xl"), lax.axis_index("z")
    me = y * 4 + xh * 2 + c
    f = xl * 4 + z
    pair = 8 * c + 2 * y + xh

    def dev(y_=y, xh_=xh, c_=c, xl_=xl, z_=z):
        return {"y": y_, "xh": xh_, "c": c_, "xl": xl_, "z": z_}

    def trial_dev(t):
        return dev(y_=t // 4, xh_=lax.rem(t // 2, 2), c_=lax.rem(t, 2))

    def feat_dev(g):
        return dev(xl_=g // 4, z_=lax.rem(g, 4))

    def plus(v, k, n):
        return lax.rem(v + k, n)

    def remote(src, dst, ss, rs, where):
        return pltpu.make_async_remote_copy(
            src_ref=src, dst_ref=dst, send_sem=ss, recv_sem=rs, device_id=where, device_id_type=MESH
        )

    z_up, z_dn = dev(z_=plus(z, 1, 4)), dev(z_=plus(z, 3, 4))
    y_up, y_dn = dev(y_=plus(y, 1, 4)), dev(y_=plus(y, 3, 4))
    across, mate, far = dev(xl_=1 - xl), dev(c_=1 - c), dev(xh_=1 - xh)
    f_up, f_dn = feat_dev(plus(f, 1, 8)), feat_dev(plus(f, 7, 8))

    chunks = TRIALS // CHUNK

    def load(i):
        k = lax.rem(i, SLOTS)
        return pltpu.make_async_copy(data.at[pl.ds(i * CHUNK, CHUNK)], raw.at[k], raw_sem.at[k])

    for i in range(SLOTS - 1):
        load(i).start()

    barrier = pltpu.get_barrier_semaphore()
    for where in (z_up, z_dn, across, f_up, f_dn):
        pl.semaphore_signal(barrier, inc=1, device_id=where, device_id_type=MESH)

    def greet(o, carry):
        pl.semaphore_signal(barrier, inc=1, device_id=trial_dev(plus(me, o, 16)), device_id_type=MESH)
        return carry

    lax.fori_loop(1, 16, greet, 0)
    pl.semaphore_wait(barrier, 20)

    lo, hi = pl.ds(0, BLOCK // 2), pl.ds(BLOCK // 2, BLOCK // 2)
    hops = [
        remote(rot, rotg.at[2], ag_s.at[0], ag_r.at[0], z_up),
        remote(rot, rotg.at[3], ag_s.at[1], ag_r.at[1], z_dn),
        remote(rot, rotg.at[1], ag_s.at[2], ag_r.at[2], across),
        remote(rotg.at[2, lo], rotg.at[4, lo], ag_s.at[3], ag_r.at[3], z_up),
        remote(rotg.at[3, hi], rotg.at[4, hi], ag_s.at[4], ag_r.at[4], z_dn),
        remote(rotg.at[1], rotg.at[5], ag_s.at[5], ag_r.at[5], z_up),
        remote(rotg.at[1], rotg.at[6], ag_s.at[6], ag_r.at[6], z_dn),
        remote(rotg.at[4, lo], rotg.at[7, lo], ag_s.at[7], ag_r.at[7], across),
        remote(rotg.at[4, hi], rotg.at[7, hi], ag_s.at[8], ag_r.at[8], across),
    ]
    for i in range(3):
        hops[i].start()

    def turn_in(i, total):
        @pl.when(i + SLOTS - 1 < chunks)
        def _():
            load(i + SLOTS - 1).start()

        load(i).wait()
        k = lax.rem(i, SLOTS)
        block = raw[k]
        wide = block.astype(F32)
        total = total + jnp.sum(wide * wide, axis=0)
        turned = jnp.swapaxes(block, 0, 1)
        rows = pl.ds(pl.multiple_of(i * CHUNK, CHUNK), CHUNK)
        for t in range(TDEV):
            dv[t // 2, rows, (t % 2) * SENS : (t % 2 + 1) * SENS] = turned[t]
        return total

    total = lax.fori_loop(0, chunks, turn_in, jnp.zeros((TDEV, SENS), F32))
    for p in range(TDEV // 2):
        lp[p] = total[2 * p : 2 * p + 2]

    def power_copy(o):
        t = plus(me, o, 16)
        theirs = 8 * lax.rem(t, 2) + t // 2
        return remote(lp.at[theirs], pw.at[o], pw_s.at[o], pw_r.at[o], trial_dev(t))

    def power_start(o, carry):
        power_copy(o).start()
        return carry

    lax.fori_loop(1, 16, power_start, 0)
    pw[0] = lp[pair]
    for slot, (dx, dz) in enumerate(AWAY):
        block = lax.rem(xl + dx, 2) * 4 + lax.rem(z + dz, 4)
        for w in range(UNITS):
            place[block * UNITS + w] = slot * UNITS + w
    rotg[0] = rot[...]

    def mate_copy(b, i):
        return remote(part.at[b, i], part_in.at[b, i], d_s.at[b, i], d_r.at[b, i], mate)

    def multiply(b, first, last):
        def body(i, carry):
            theirs = plus(y, lax.rem(3 * (i // 2) + 2, 4), 4) * 2 + lax.rem(i, 2)
            for half in (1 - c, c):
                left = rotg[4 * b : 4 * b + 4].reshape(BATCH, TRIALS)
                sums = jnp.dot(left, dv[8 * half + theirs], preferred_element_type=F32)
                if half is c:
                    acc[b, i] = sums
                else:
                    part[b, i] = sums
                    mate_copy(b, i).start()
            return carry

        lax.fori_loop(first, last, body, 0)

    def relay_copies(b, side, h):
        where = (y_up, y_dn)[side]
        return (
            remote(s1.at[b, side, h], r1.at[b, side, h], r1_s.at[b, side, h, 0], r1_r.at[b, side, h, 0], where),
            remote(s1s.at[b, side, h], r1s.at[b, side, h], r1_s.at[b, side, h, 1], r1_r.at[b, side, h, 1], where),
        )

    def owner_copies(b, side, h):
        where = (y_up, y_dn)[side]
        return (
            remote(s2.at[b, side, h], r2.at[b, side, h], r2_s.at[b, side, h, 0], r2_r.at[b, side, h, 0], where),
            remote(s2s.at[b, side, h], r2s.at[b, side, h], r2_s.at[b, side, h, 1], r2_r.at[b, side, h, 1], where),
        )

    def far_copies(b):
        return (
            remote(sx.at[b], rx.at[b], x_s.at[b, 0], x_r.at[b, 0], far),
            remote(sxs.at[b], rxs.at[b], x_s.at[b, 1], x_r.at[b, 1], far),
        )

    def start(copies):
        for copy in copies:
            copy.start()

    def arrive(copies):
        for copy in copies:
            copy.wait_recv()

    def rows_of(k):
        return pl.ds(k * BLOCK, BLOCK)

    def units_of(b, k):
        return pl.ds((4 * b + k) * UNITS, UNITS)

    def chip_sum(b, i, k):
        return acc[b, i, rows_of(k)] + part_in[b, i, rows_of(k)]

    def relay(b):
        for h in range(2):
            mate_copy(b, h).wait_recv()
            for side in range(2):
                for k in range(2):
                    encode(
                        chip_sum(b, h, 2 * side + k),
                        functools.partial(s1.__setitem__, (b, side, h, rows_of(k))),
                        functools.partial(s1s.__setitem__, (b, side, h, k)),
                    )
                start(relay_copies(b, side, h))

    def to_owner(b, side):
        for h in range(2):
            i = (2, 6)[side] + h
            mate_copy(b, i).wait_recv()
            arrive(relay_copies(b, side, h))
            for k in range(4):
                v = chip_sum(b, i, k)
                if k // 2 == side:
                    v = v + decode(r1[b, side, h, rows_of(k % 2)], r1s[b, side, h, k % 2])
                encode(
                    v,
                    functools.partial(s2.__setitem__, (b, side, h, rows_of(k))),
                    functools.partial(s2s.__setitem__, (b, side, h, k)),
                )
            start(owner_copies(b, side, h))

    def own(b, i, h, k):
        v = chip_sum(b, i, k)
        for side in range(2):
            v = v + decode(r2[b, side, h, rows_of(k)], r2s[b, side, h, k])
        return v

    def to_far(b):
        for h in range(2):
            mate_copy(b, 4 + h).wait_recv()
            for side in range(2):
                arrive(owner_copies(b, side, h))
        for k in range(4):
            encode(
                own(b, 5 - xh, 1 - xh, k),
                functools.partial(sx.__setitem__, (b, rows_of(k))),
                functools.partial(sxs.__setitem__, (b, k)),
            )
        start(far_copies(b))
        for k in range(4):
            fin[units_of(b, k)] = own(b, 4 + xh, xh, k).reshape(UNITS, 16, 2 * SENS)

    def finish(b):
        arrive(far_copies(b))
        for k in range(4):
            at = units_of(b, k)
            fin[at] = fin[at] + decode(rx[b, rows_of(k)], rxs[b, k]).reshape(UNITS, 16, 2 * SENS)

    for i in range(3):
        hops[i].wait_recv()
    for i in range(3, 7):
        hops[i].start()
    multiply(0, 0, 4)
    relay(0)
    for i in (3, 4):
        hops[i].wait_recv()
        hops[i + 4].start()
    multiply(0, 4, 8)
    to_owner(0, 0)
    to_owner(0, 1)
    for i in range(5, 9):
        hops[i].wait_recv()
    multiply(1, 0, 4)
    relay(1)
    to_far(0)
    multiply(1, 4, 8)
    to_owner(1, 0)
    to_owner(1, 1)
    finish(0)
    to_far(1)

    def power_wait(o, carry):
        power_copy(o).wait_recv()
        return carry

    lax.fori_loop(1, 16, power_wait, 0)
    power = jnp.sum(pw[...], axis=0) * (1.0 / (TRIALS * 16))
    scale = 1.0 / jnp.sqrt(power + 1e-05)
    scale = jnp.concatenate([scale[0:1], scale[1:2]], axis=1)
    finish(1)

    def unit_of(u):
        return place[8 * order[u // 8] + lax.rem(u, 8)]

    mine = pl.ds(2 * pair, 2)

    def score_copies(o):
        where = trial_dev(plus(me, o, 16))
        return (
            remote(a2s.at[o], a2r.at[mine], a_s.at[o, 0], a_r.at[o, 0], where),
            remote(a2ss.at[o], a2rs.at[mine], a_s.at[o, 1], a_r.at[o, 1], where),
        )

    def pick(o):
        t = plus(me, o, 16)
        v = jnp.concatenate([fin[unit_of(3 * t + j)] for j in range(3)], axis=0) * scale

        def put(to, q):
            to[0] = q[:, :SENS]
            to[1] = q[:, SENS:]

        return v, put

    def score_start(o, carry):
        v, put = pick(o)
        encode(v, functools.partial(put, a2s.at[o]), functools.partial(put, a2ss.at[o]))
        start(score_copies(o))
        return carry

    lax.fori_loop(1, 16, score_start, 0)
    v, put = pick(0)
    encode(v, functools.partial(put, a2r.at[mine]), functools.partial(put, a2rs.at[mine]))

    links = adj[...].astype(F32)
    at = (lax.broadcasted_iota(jnp.int32, (SENS, SENS), 0), lax.broadcasted_iota(jnp.int32, (SENS, SENS), 1))
    joined = (links + jnp.where(at[0] == at[1], 1.0, 0.0)).astype(BF16)
    contract = (((1,), (1,)), ((), ()))
    degree = lax.dot_general(jnp.ones((8, SENS), BF16), joined, contract, preferred_element_type=F32)
    share = 1.0 / degree[0:1]

    def score_wait(o, carry):
        arrive(score_copies(o))
        return carry

    lax.fori_loop(1, 16, score_wait, 0)
    edge = [
        remote(a2r.at[pl.ds(TDEV - 4, 4)], hr.at[0], h_s.at[0], h_r.at[0], f_up),
        remote(a2rs.at[pl.ds(TDEV - 4, 4)], hrs.at[0], h_s.at[1], h_r.at[1], f_up),
        remote(a2r.at[pl.ds(0, 4)], hr.at[1], h_s.at[2], h_r.at[2], f_dn),
        remote(a2rs.at[pl.ds(0, 4)], hrs.at[1], h_s.at[3], h_r.at[3], f_dn),
    ]
    start(edge)

    def mixed(q, s):
        v = decode(q, s)
        square = (v * v).reshape(4 * OWNED, SENS)
        head = square.astype(BF16)
        rest = (square - head.astype(F32)).astype(BF16)
        both = lax.dot_general(head, joined, contract, preferred_element_type=F32) + lax.dot_general(
            rest, joined, contract, preferred_element_type=F32
        )
        return (both * share).reshape(4, OWNED, SENS)

    def mix_step(i, carry):
        four = pl.ds(4 * i, 4)
        spread[pl.ds(4 * i + 4, 4)] = mixed(a2r[four], a2rs[four])
        return carry

    lax.fori_loop(0, TDEV // 4, mix_step, 0)
    arrive(edge)
    spread[0:4] = jnp.where(f > 0, mixed(hr[0], hrs[0]), 0.0)
    spread[TDEV + 4 : TDEV + 8] = jnp.where(f < 7, mixed(hr[1], hrs[1]), 0.0)

    def smooth(i, carry):
        for j in range(8):
            line = jnp.zeros((OWNED, SENS), F32)
            for k in range(9):
                line = line + taps[k] * spread[8 * i + j + k]
            turn[j] = line
        out[:, pl.ds(pl.multiple_of(8 * i, 8), 8), :] = jnp.swapaxes(turn[...], 0, 1)
        return carry

    lax.fori_loop(0, TDEV // 8, smooth, 0)

    for hop in hops:
        hop.wait_send()

    def gone(o, carry):
        power_copy(o).wait_send()
        for copy in score_copies(o):
            copy.wait_send()
        return carry

    lax.fori_loop(1, 16, gone, 0)
    for b in range(2):
        for i in range(8):
            mate_copy(b, i).wait_send()
        for side in range(2):
            for h in range(2):
                for copy in relay_copies(b, side, h) + owner_copies(b, side, h):
                    copy.wait_send()
        for copy in far_copies(b):
            copy.wait_send()
    for copy in edge:
        copy.wait_send()


def per_device(data, rotations, span_order, adjacency, taps):
    vmem, smem, dma = pltpu.VMEM, pltpu.SMEM, pltpu.SemaphoreType.DMA
    spec = lambda space: pl.BlockSpec(memory_space=space)
    wide = 2 * SENS
    scratch = [
        vmem((SLOTS, CHUNK, TDEV, SENS), BF16),
        vmem((TDEV // 2, TRIALS, wide), BF16),
        vmem((8, BLOCK, TRIALS), BF16),
        vmem((16, 2, SENS), F32),
        vmem((16, 2, SENS), F32),
        vmem((2, 8, BATCH, wide), F32),
        vmem((2, 8, BATCH, wide), F32),
        vmem((2, 8, BATCH, wide), F32),
        vmem((2, 2, 2, BATCH // 2, wide), I16),
        vmem((2, 2, 2, 2, 1, wide), F32),
        vmem((2, 2, 2, BATCH // 2, wide), I16),
        vmem((2, 2, 2, 2, 1, wide), F32),
        vmem((2, 2, 2, BATCH, wide), I16),
        vmem((2, 2, 2, 4, 1, wide), F32),
        vmem((2, 2, 2, BATCH, wide), I16),
        vmem((2, 2, 2, 4, 1, wide), F32),
        vmem((2, BATCH, wide), I16),
        vmem((2, 4, 1, wide), F32),
        vmem((2, BATCH, wide), I16),
        vmem((2, 4, 1, wide), F32),
        vmem((8 * UNITS, 16, wide), F32),
        smem((8 * UNITS,), jnp.int32),
        vmem((16, 2, OWNED, SENS), I16),
        vmem((16, 2, 1, SENS), F32),
        vmem((TDEV, OWNED, SENS), I16),
        vmem((TDEV, 1, SENS), F32),
        vmem((2, 4, OWNED, SENS), I16),
        vmem((2, 4, 1, SENS), F32),
        vmem((TDEV + 8, OWNED, SENS), F32),
        vmem((8, OWNED, SENS), F32),
        dma((SLOTS,)),
        dma((9,)), dma((9,)),
        dma((16,)), dma((16,)),
        dma((2, 8)), dma((2, 8)),
        dma((2, 2, 2, 2)), dma((2, 2, 2, 2)),
        dma((2, 2, 2, 2)), dma((2, 2, 2, 2)),
        dma((2, 2)), dma((2, 2)),
        dma((16, 2)), dma((16, 2)),
        dma((4,)), dma((4,)),
    ]
    return pl.pallas_call(
        kernel,
        out_shape=jax.ShapeDtypeStruct((OWNED, TDEV, SENS), F32),
        in_specs=[spec(smem), spec(smem), spec(pl.ANY), spec(vmem), spec(vmem)],
        out_specs=spec(vmem),
        scratch_shapes=scratch,
        compiler_params=pltpu.CompilerParams(
            collective_id=0, has_side_effects=True, vmem_limit_bytes=66000000
        ),
    )(span_order, taps, data, rotations, adjacency)


def solution(mesh):
    torus = Mesh(mesh.devices.reshape(4, 2, 2, 2, 4), TRIAL + FEAT)
    in_specs = (P(TRIAL, FEAT, None), P(FEAT, TRIAL), P(), P(), P())
    return jax.shard_map(
        per_device, mesh=torus, in_specs=in_specs, out_specs=P(TRIAL, FEAT, None), check_vma=False
    )
```

time: 230 us -> 88.3 us (0.38)
  the two profiles are of different devices: /device:TPU:2 before, /device:TPU:1 now
where the time goes in v1:
time: 88.3 us; the launch traced here: 88.1 us
  Pallas kernels  86 us (97%)
  local copies, waits for them, and re-layouts  2.06 us (2%)
    pallas_call x1, Pallas kernels, per_device(): pl.pallas_call(kernel, out_shape=jax.ShapeDtypeStruct((OWNED, TDEV, SENS)...  86 us
    unnamed x1, local copies, waits for them, and re-layouts  2.06 us

profile of v1, /device:TPU:1, one launch (start us, length us, event | category | flops | bytes accessed | tf_op | source)
XLA Modules:
  0.0 88.1 jit_solution(8957937082690301001)
XLA Ops:
  0.0 86.0 %shard_map.55 = f32[48,32,128]{2,1,0:T(8,128)} custom-call(s32[6]{0:T(128)} %order.1, f32[9]{0:T(128)} %taps.1, bf16[2048,32,128]{2,1,0:T(8,128)(2,1)} %data.1, bf16[96,2048]{1,0:T(8,128)(2,1)} %rot.1, s32[128,128]{1,0:T(8,128)} %adj.1), custom_call_target="tpu_custom_call" | custom-call | tf_op jit(solution)/shard_map/pallas_call | solution.py:435
  86.0 2.1 %copy.7 = f32[48,32,128]{2,1,0:T(8,128)} copy(f32[48,32,128]{2,1,0:T(8,128)} %shard_map.55) | data formatting | bytes 1572864
